TPU v7x, 256 devices: a whole 4x4x8 slice. The times are simulated.
256 devices in a mesh: seq: 16 (over z, core), tp: 8 (over x_lo, y), dp: 2 (over x_hi).
Axes of the slice: x: 4 (x_hi: 2, x_lo: 2; x = x_hi * 2 + x_lo), y: 4, z: 8, core: 2. Of those that a mesh axis runs over, the one named last changes fastest.
Arguments:
- query_latent: bfloat16 [2, 4096, 1536], P('dp', 'seq', 'tp'), may hold values from -6 to 6
- key_latent: bfloat16 [2, 4096, 512], P('dp', 'seq', 'tp'), may hold values from -6 to 6
- rope_key: bfloat16 [2, 4096, 64], P('dp', 'seq'), may hold values from -6 to 6
- w_uq: bfloat16 [1536, 12288], P('seq', 'tp')
- w_uk: bfloat16 [512, 8192], P('seq', 'tp'), may hold values from -0.25 to 0.25
- w_uv: bfloat16 [512, 8192], P('seq', 'tp'), may hold values from -0.25 to 0.25
- block_order: int32 [2, 32], P('dp'), may hold values from 0 to 31, each once within a row
- segment_ids: int32 [2, 4096], P('dp'), may hold values from 0 to 3, never falling along the last dimension, each value on 1 to 2048 neighbouring positions
Outputs:
- context: bfloat16 [2, 4096, 8192], P('dp', 'seq', 'tp')
- clipped_uq: bfloat16 [1536, 12288], P('seq', 'tp')
- clipped_uk: bfloat16 [512, 8192], P('seq', 'tp')
Inputs may be any that keep to these rules, and one draw needn't show every extreme that they name: `block_order`: each row is a permutation of the 32 position blocks. `segment_ids`: never falling along positions; each document has at most 2048 positions.
All inputs are finite; a program needn't handle non-finite values.
Results may differ from a plain program's by a relative error of at most 0.012.
The roundings to bfloat16 on the way count: a program that leaves them out, or rounds other values in their place, can miss the bound.
Values may be sent and summed in bfloat16 or wider, within the bound.
A program may use at most 64 MiB of HBM per device.

v0:
```python
import math

import jax
import jax.numpy as jnp
from jax import lax
from jax.sharding import PartitionSpec as P

NOPE = 128
ROPE = 64
VD = 128
CLIP = 8


rope_base = 50000.0
masked_value = -1e30


def in_one_piece(arrays, axis, dim, along):
    both = jnp.concatenate(arrays, axis=along)
    whole, at, gathered = (lax.all_gather(both, axis, axis=dim, tiled=True), 0, [])
    for a in arrays:
        gathered.append(lax.slice_in_dim(whole, at, at + a.shape[along], axis=along))
        at += a.shape[along]
    return tuple(gathered)


def copy_for_each(array, axis):
    copies = jnp.broadcast_to(array, (lax.axis_size(axis), *array.shape))
    return lax.all_to_all(copies, axis, split_axis=0, concat_axis=0, tiled=True)


def of_everyone(array, axis):
    everything = copy_for_each(array, axis)
    return jnp.max(everything, axis=0)


def turning(positions, width):
    steps = jnp.arange(width // 2, dtype=jnp.float32) * (2.0 / width)
    freqs = jnp.exp(-math.log(rope_base) * steps)
    angle = positions.astype(jnp.float32)[:, None] * freqs[None, :]
    return (jnp.cos(angle), jnp.sin(angle))


def rotate(values, cosine, sine):
    half = values.shape[-1] // 2
    first = values[..., :half]
    second = values[..., half:]
    return jnp.concatenate(
        [first * cosine - second * sine, second * cosine + first * sine], axis=-1
    )


def positions_of(index, order, half_block):
    which = index // half_block
    onehot = which[:, None] == jnp.arange(order.shape[0], dtype=jnp.int32)[None, :]
    base = jnp.sum(jnp.where(onehot, order[None, :], 0), axis=1)
    return base * half_block + index % half_block


def on_device(query_latent, key_latent, rope_key, w_uq, w_uk, w_uv, block_order, segment_ids):
    query_local, key_local = (
        lax.all_gather(query_latent[0], "tp", axis=1, tiled=True),
        lax.all_gather(key_latent[0], "tp", axis=1, tiled=True),
    )
    rows_uq, rows_uk, rows_uv = (
        lax.all_gather(w_uq, "seq", axis=0, tiled=True),
        *in_one_piece((w_uk, w_uv), "seq", 0, 1),
    )
    tok_rows = query_local.shape[0]
    half_block = tok_rows // 2
    order = block_order[0]
    labels_all = segment_ids[0]
    heads = w_uq.shape[1] // (NOPE + ROPE)
    scale = 1.0 / math.sqrt(NOPE + ROPE)
    own_index = lax.axis_index("seq") * tok_rows + jnp.arange(tok_rows, dtype=jnp.int32)
    query_pos = positions_of(own_index, order, half_block)
    query_labels = jnp.take(labels_all, query_pos)
    cosine, sine = turning(query_pos, ROPE)
    query_full = jnp.dot(query_local, rows_uq, preferred_element_type=jnp.float32).reshape(
        tok_rows, heads, NOPE + ROPE
    )
    query_nope = jnp.transpose(query_full[:, :, :NOPE].astype(jnp.bfloat16), (1, 0, 2))
    query_rope = jnp.transpose(
        rotate(query_full[:, :, NOPE:], cosine[:, None, :], sine[:, None, :]).astype(jnp.bfloat16),
        (1, 0, 2),
    )
    key_rope = rotate(rope_key[0].astype(jnp.float32), cosine, sine).astype(jnp.bfloat16)

    def slice_latent(pieces, first, width):
        latent_block = lax.dynamic_slice_in_dim(pieces[0], first, width, 0)
        rope_block = lax.dynamic_slice_in_dim(pieces[1], first, width, 0)
        nope_block = jnp.dot(latent_block, rows_uk, preferred_element_type=jnp.float32).astype(
            jnp.bfloat16
        )
        value_block = jnp.dot(latent_block, rows_uv, preferred_element_type=jnp.float32).astype(
            jnp.bfloat16
        )
        return (nope_block, value_block, rope_block)

    initial = (
        jnp.full((heads, tok_rows), masked_value, jnp.float32),
        jnp.zeros((heads, tok_rows), jnp.float32),
        jnp.zeros((heads, tok_rows, VD), jnp.float32),
    )
    pieces = in_one_piece((key_local, key_rope), "seq", 0, 1)
    count = pieces[-1].shape[0]
    width = math.gcd(count, 512)

    def block_step(state, number):
        first = number * width
        nope_block, value_block, rope_block = slice_latent(pieces, first, width)
        nope_block = nope_block.reshape(width, heads, NOPE)
        value_block = value_block.reshape(width, heads, VD)
        key_index = first + jnp.arange(width, dtype=jnp.int32)
        key_pos = positions_of(key_index, order, half_block)
        key_labels = jnp.take(labels_all, key_pos)
        allowed = (key_pos[None, :] <= query_pos[:, None]) & (
            key_labels[None, :] == query_labels[:, None]
        )
        scores = jnp.einsum(
            "hqd,khd->hqk", query_nope, nope_block, preferred_element_type=jnp.float32
        )
        scores = (
            scores
            + jnp.einsum("hqr,kr->hqk", query_rope, rope_block, preferred_element_type=jnp.float32)
        ) * scale
        masked = jnp.where(allowed[None], scores, masked_value)
        run_max, run_total, run_sum = state
        new_max = jnp.maximum(run_max, jnp.max(masked, axis=2))
        weights = jnp.where(allowed[None], jnp.exp(masked - new_max[:, :, None]), 0.0)
        shrink = jnp.exp(run_max - new_max)
        new_total = run_total * shrink + jnp.sum(weights, axis=2)
        mixed = jnp.einsum(
            "hqk,khv->hqv",
            weights.astype(jnp.bfloat16),
            value_block,
            preferred_element_type=jnp.float32,
        )
        new_sum = run_sum * shrink[:, :, None] + mixed
        return ((new_max, new_total, new_sum), None)

    result, unused = lax.scan(block_step, initial, jnp.arange(count // width, dtype=jnp.int32))
    run_max, run_total, run_sum = result
    context = (run_sum / run_total[:, :, None]).astype(jnp.bfloat16)
    context = jnp.transpose(context, (1, 0, 2)).reshape(1, tok_rows, heads * VD)
    head_max = of_everyone(jnp.max(run_max, axis=1), ("seq", "dp"))
    ratio = CLIP / jnp.maximum(head_max, CLIP)
    root = jnp.sqrt(ratio)
    factors = jnp.concatenate(
        [
            jnp.broadcast_to(root[:, None], (heads, NOPE)),
            jnp.broadcast_to(ratio[:, None], (heads, ROPE)),
        ],
        axis=1,
    ).reshape(heads * (NOPE + ROPE))
    clipped_uq = (w_uq.astype(jnp.float32) * factors[None, :]).astype(jnp.bfloat16)
    clipped_uk = (w_uk.astype(jnp.float32) * jnp.repeat(root, NOPE)[None, :]).astype(jnp.bfloat16)
    return (context, clipped_uq, clipped_uk)


def solution(mesh):
    placed = (
        P("dp", "seq", "tp"),
        P("dp", "seq", "tp"),
        P("dp", "seq", None),
        P("seq", "tp"),
        P("seq", "tp"),
        P("seq", "tp"),
        P("dp", None),
        P("dp", None),
    )
    return jax.shard_map(
        on_device,
        mesh=mesh,
        in_specs=placed,
        out_specs=(P("dp", "seq", "tp"), P("seq", "tp"), P("seq", "tp")),
        check_vma=False,
    )
```

profile of v0, /device:TPU:1, one launch (start us, length us, event | category | flops | bytes accessed | tf_op | source)
XLA Modules:
  0.0 318.9 jit_solution(3619751761167049649)
XLA Ops:
  10.4 24.1 %all-gather = bf16[1,256,512]{1,2,0:T(8,128)(2,1)S(1)} all-gather(bf16[1,256,64]{1,2,0:T(8,128)(2,1)} %param.11), channel_id=2, replica_groups=mesh['seq'=16,'tp'=8,'dp'=2] {'tp'}, dimensions={2}, use_global_device_ids=true | all-gather | bytes 294912 | tf_op jit(solution)/shard_map/all_gather | solution.py:63
  38.2 24.7 %all-gather.1 = bf16[1,256,1536]{1,2,0:T(8,128)(2,1)S(1)} all-gather(bf16[1,256,192]{1,2,0:T(8,128)(2,1)} %param.10), channel_id=3, replica_groups=mesh['seq'=16,'tp'=8,'dp'=2] {'tp'}, dimensions={2}, use_global_device_ids=true | all-gather | bytes 884736 | tf_op jit(solution)/shard_map/all_gather | solution.py:62
  62.9 3.2 fusion.47
  66.0 30.5 %all-gather.10.cloned.1.call-done = bf16[1536,1536]{1,0:T(8,128)(2,1)} async-done(((bf16[96,1536]{1,0:T(8,128)(2,1)}), bf16[1536,1536]{1,0:T(8,128)(2,1)}) %all-gather.10.cloned.1.call-update) | async-done | bytes 4718608 | tf_op jit(solution)/shard_map/all_gather | solution.py:66
  96.5 4.3 %fusion.34 = f32[256,1536]{0,1:T(8,128)S(1)} fusion(bf16[1536,1536]{1,0:T(8,128)(2,1)} %all-gather.10.cloned.1.call-done, bf16[1,256,1536]{1,2,0:T(8,128)(2,1)S(1)} %all-gather.1), kind=kOutput, calls=%fused_computation.61 | convolution fusion | flops 1207959552 | bytes 7077888 | tf_op jit(solution)/shard_map/dot_general | solution.py:79
  103.5 46.1 %all-gather.6.cloned.1.call-done = bf16[4096,576]{0,1:T(8,128)(2,1)} async-done(((bf16[256,576]{0,1:T(8,128)(2,1)}), bf16[4096,576]{0,1:T(8,128)(2,1)}) %all-gather.6.cloned.1.call-update) | async-done | bytes 4718608 | tf_op jit(solution)/shard_map/all_gather | solution.py:20
  149.6 4.8 %slice.46 = bf16[4096,512]{0,1:T(8,128)(2,1)} slice(bf16[4096,576]{0,1:T(8,128)(2,1)} %all-gather.6.cloned.1.call-done), slice={[0:4096], [0:512]} | slice | bytes 8388608 | tf_op jit(solution)/shard_map/slice | solution.py:22
  154.4 139.5 %while.17 = (s32[]{:T(128)}, f32[8,256]{1,0:T(8,128)S(1)}, f32[8,256]{1,0:T(8,128)S(1)}, f32[8,256,128]{2,1,0:T(8,128)S(1)}, s32[8]{0:T(128)S(1)}, /*index=5*/s3...) while((s32[]{:T(128)}, f32[8,256]{1,0:T(8,128)S(1)}, ...), condition=%wide.region_5.6_spmd.clone, body=%wide.region_1.5_spmd.clone.sunk | while | flops 1757632000 | bytes 48734628 | solution.py:142
  155.8 3.1 gather_fusion
  162.0 3.0 fusion.80
  165.0 3.1 fusion.81
  173.2 3.1 gather_fusion
  179.5 3.0 fusion.80
  182.4 3.1 fusion.81
  190.7 3.1 gather_fusion
  196.9 3.0 fusion.80
  199.9 3.1 fusion.81
  208.1 3.1 gather_fusion
  214.3 3.0 fusion.80
  217.3 3.1 fusion.81
  225.6 3.1 gather_fusion
  231.8 3.0 fusion.80
  234.8 3.1 fusion.81
  243.0 3.1 gather_fusion
  249.2 3.0 fusion.80
  252.2 3.1 fusion.81
  260.4 3.1 gather_fusion
  269.6 3.1 fusion.81
  277.9 3.1 gather_fusion
  287.1 3.1 fusion.81
  294.7 6.6 %all-to-all-start = ((f32[32,1,8]{2,1,0:T(1,128)}), f32[32,1,8]{2,1,0:T(1,128)S(1)}, u32[]{:S(2)}, u32[]{:S(2)}) async-start(f32[32,1,8]{2,1,0:T(1,128)} %broadcast_in_dim.126), calls=%async_computation | async-start | bytes 32768 | tf_op jit(solution)/shard_map/all_to_all | solution.py:29
  303.0 7.6 %all-to-all-done = f32[32,1,8]{2,1,0:T(1,128)S(1)} async-done(((f32[32,1,8]{2,1,0:T(1,128)}), f32[32,1,8]{2,1,0:T(1,128)S(1)}, u32[]{:S(2)}, u32[]{:S(2)}) %all-to-all-start) | async-done | bytes 1056 | tf_op jit(solution)/shard_map/all_to_all | solution.py:29
  (191 shorter events, 79.6 us)
Async XLA Ops:
  7.2 55.7 %all-gather.8.cloned.1.call-start = ((), (), s32[]{:S(2)}) async-start(), calls=%async_computation.2 | async-start | bytes 2228224 | tf_op jit(solution)/shard_map/all_gather | solution.py:20
  8.8 87.7 %all-gather.10.cloned.1.call-start = ((), (), s32[]{:S(2)}) async-start(), calls=%async_computation.3 | async-start | bytes 5013504 | tf_op jit(solution)/shard_map/all_gather | solution.py:66
  9.5 140.1 %all-gather.6.cloned.1.call-start = ((), (), s32[]{:S(2)}) async-start(), calls=%async_computation.1 | async-start | bytes 5013504 | tf_op jit(solution)/shard_map/all_gather | solution.py:20
  100.8 1.2 copy-start.3
  103.4 50.9 %copy-start = (s32[1,4096]{1,0:T(1,128)S(1)}, s32[1,4096]{1,0:T(1,128)}, u32[]{:S(2)}) copy-start(s32[1,4096]{1,0:T(1,128)} %param.17) | copy-start | bytes 49156
  103.4 50.9 %copy-start.5 = (s32[1,32]{1,0:T(1,128)S(1)}, s32[1,32]{1,0:T(1,128)}, u32[]{:S(2)}) copy-start(s32[1,32]{1,0:T(1,128)} %param.16) | copy-start | bytes 388
  149.6 4.8 %slice-start = ((bf16[4096,576]{0,1:T(8,128)(2,1)}), bf16[4096,64]{0,1:T(8,128)(2,1)S(1)}, s32[]{:S(2)}) async-start(bf16[4096,576]{0,1:T(8,128)(2,1)} %all-gather.6.cloned.1.call-done), calls=%async_computation.4 | async-start | bytes 1048576 | tf_op jit(solution)/shard_map/slice | solution.py:22
  154.4 156.6 %copy-start.2 = (bf16[96,1536]{1,0:T(8,128)(2,1)S(1)}, bf16[96,1536]{1,0:T(8,128)(2,1)}, u32[]{:S(2)}) copy-start(bf16[96,1536]{1,0:T(8,128)(2,1)} %param.13) | copy-start | bytes 884740
  165.0 5.2 %copy-start.1 = (f32[8,256,512]{1,2,0:T(8,128)S(1)}, f32[8,256,512]{1,2,0:T(8,128)}, u32[]{:S(2)}) copy-start(f32[8,256,512]{1,2,0:T(8,128)} %get-tuple-element.455) | copy-start | bytes 12582916 | tf_op jit(solution)/shard_map/while
  182.4 5.2 %copy-start.1 = (f32[8,256,512]{1,2,0:T(8,128)S(1)}, f32[8,256,512]{1,2,0:T(8,128)}, u32[]{:S(2)}) copy-start(f32[8,256,512]{1,2,0:T(8,128)} %get-tuple-element.455) | copy-start | bytes 12582916 | tf_op jit(solution)/shard_map/while
  199.9 5.2 %copy-start.1 = (f32[8,256,512]{1,2,0:T(8,128)S(1)}, f32[8,256,512]{1,2,0:T(8,128)}, u32[]{:S(2)}) copy-start(f32[8,256,512]{1,2,0:T(8,128)} %get-tuple-element.455) | copy-start | bytes 12582916 | tf_op jit(solution)/shard_map/while
  217.3 5.2 %copy-start.1 = (f32[8,256,512]{1,2,0:T(8,128)S(1)}, f32[8,256,512]{1,2,0:T(8,128)}, u32[]{:S(2)}) copy-start(f32[8,256,512]{1,2,0:T(8,128)} %get-tuple-element.455) | copy-start | bytes 12582916 | tf_op jit(solution)/shard_map/while
  234.8 5.2 %copy-start.1 = (f32[8,256,512]{1,2,0:T(8,128)S(1)}, f32[8,256,512]{1,2,0:T(8,128)}, u32[]{:S(2)}) copy-start(f32[8,256,512]{1,2,0:T(8,128)} %get-tuple-element.455) | copy-start | bytes 12582916 | tf_op jit(solution)/shard_map/while
  252.2 5.2 %copy-start.1 = (f32[8,256,512]{1,2,0:T(8,128)S(1)}, f32[8,256,512]{1,2,0:T(8,128)}, u32[]{:S(2)}) copy-start(f32[8,256,512]{1,2,0:T(8,128)} %get-tuple-element.455) | copy-start | bytes 12582916 | tf_op jit(solution)/shard_map/while
  269.6 5.2 %copy-start.1 = (f32[8,256,512]{1,2,0:T(8,128)S(1)}, f32[8,256,512]{1,2,0:T(8,128)}, u32[]{:S(2)}) copy-start(f32[8,256,512]{1,2,0:T(8,128)} %get-tuple-element.455) | copy-start | bytes 12582916 | tf_op jit(solution)/shard_map/while
  287.1 5.2 %copy-start.1 = (f32[8,256,512]{1,2,0:T(8,128)S(1)}, f32[8,256,512]{1,2,0:T(8,128)}, u32[]{:S(2)}) copy-start(f32[8,256,512]{1,2,0:T(8,128)} %get-tuple-element.455) | copy-start | bytes 12582916 | tf_op jit(solution)/shard_map/while
  293.9 17.8 %copy-start.4 = (bf16[32,1024]{1,0:T(8,128)(2,1)S(1)}, bf16[32,1024]{1,0:T(8,128)(2,1)}, u32[]{:S(2)}) copy-start(bf16[32,1024]{1,0:T(8,128)(2,1)} %param.14) | copy-start | bytes 196612
  294.7 15.9 %all-to-all-start = ((f32[32,1,8]{2,1,0:T(1,128)}), f32[32,1,8]{2,1,0:T(1,128)S(1)}, u32[]{:S(2)}, u32[]{:S(2)}) async-start(f32[32,1,8]{2,1,0:T(1,128)} %broadcast_in_dim.126), calls=%async_computation | async-start | bytes 32768 | tf_op jit(solution)/shard_map/all_to_all | solution.py:29
Sparse Core Ops, SparseCore 0:
  10.4 43.6 all-gather.7
  55.9 40.5 all-gather.9
  98.8 50.7 all-gather.5
where the time goes:
time: 320 us; the launch traced here: 319 us
  waiting for transfers between devices  84.9 us (27%)
  matrix products  80.3 us (25%)
  blocking collectives  48.7 us (15%)
  local copies, waits for them, and re-layouts  43.6 us (14%)
  other arithmetic  34.6 us (11%)
  between operations  13.9 us (4%)
  starting transfers between devices  6.74 us (2%)
  loops' own time  6.11 us (2%)
    all_gather x2, waiting for transfers between devices, in_one_piece(): lax.all_gather(both, axis, axis=dim, tiled=True)  46.1 us
    all_gather x1, waiting for transfers between devices, on_device(): lax.all_gather(w_uq, 'seq', axis=0, tiled=True)  30.5 us
    gather x8, local copies, waits for them, and re-layouts, block_step(): key_labels = jnp.take(labels_all, key_pos)  25.1 us
    all_gather x1, blocking collectives, on_device(): lax.all_gather(query_latent[0], 'tp', axis=1, tiled=True)  24.7 us
    reduce_sum x8, other arithmetic, block_step(): new_total = run_total * shrink + jnp.sum(weights, axis=2)  24.5 us
    all_gather x1, blocking collectives, on_device(): lax.all_gather(key_latent[0], 'tp', axis=1, tiled=True)  24.1 us
    dot_general x8, matrix products, block_step(): jnp.einsum('hqr,kr->hqk', query_rope, rope_block, preferred_element_type=...  23.8 us
    dot_general x8, matrix products, slice_latent(): jnp.dot(latent_block, rows_uv, preferred_element_type=jnp.float32)  17 us
  transfers between devices with their start and end apart: 4, of which 3 were waited for; matrix products, arithmetic and copies ran while one was open for 5% of the time, Pallas kernels for 0%

commit v1 on v0

v1 whole, which is shorter than its diff:
```python
import functools
import math

import jax
import jax.numpy as jnp
from jax import lax
from jax.experimental import pallas as pl
from jax.experimental.pallas import tpu as pltpu
from jax.sharding import PartitionSpec as P

NOPE = 128
ROPE = 64
VD = 128
CLIP = 8
NZ = 8
NY = 4
NX = 2
NTP = NX * NY
BLK = 128
MIB = 1 << 20

rope_base = 50000.0
masked_value = -1e30
MESH = pl.DeviceIdType.MESH
F32 = jnp.float32
BF16 = jnp.bfloat16


def cos_sin(angle):
    k = jnp.floor(angle * (2.0 / math.pi) + 0.5)
    r = angle - k * 1.5703125
    r = r - k * 4.837512969970703125e-4
    r = r - k * 7.54978995489188216e-8
    z = r * r
    s = ((-1.9515295891e-4 * z + 8.3321608736e-3) * z - 1.6666654611e-1) * z * r + r
    c = (
        ((2.443315711809948e-5 * z - 1.388731625493765e-3) * z + 4.166664568298827e-2) * z * z
        - 0.5 * z
        + 1.0
    )
    q = k - 4.0 * jnp.floor(k * 0.25)
    odd = (q == 1.0) | (q == 3.0)
    sine = jnp.where(odd, c, s)
    cosine = jnp.where(odd, s, c)
    sine = jnp.where(q >= 2.0, -sine, sine)
    cosine = jnp.where((q == 1.0) | (q == 2.0), -cosine, cosine)
    return cosine, sine


def turning(pos, lane):
    step = lax.rem(lane, ROPE // 2).astype(F32) * (2.0 / ROPE)
    freq = jnp.exp(-math.log(rope_base) * step)
    cosine, sine = cos_sin(pos.astype(F32) * freq)
    sine = jnp.where(lax.rem(lane, ROPE) < ROPE // 2, -sine, sine)
    return cosine, sine


def swapped(x):
    h = ROPE // 2
    return jnp.concatenate(
        [x[:, h : 2 * h], x[:, :h], x[:, 3 * h : 4 * h], x[:, 2 * h : 3 * h]], axis=1
    )


def folded(x):
    n = x.shape[0] // 2
    return jnp.concatenate([x[:n], x[n:]], axis=1)


def gather_kernel(
    order, rope_ref, key_ref, query_hbm, uq_hbm, uk_hbm, uv_hbm,
    k_out, vt_out, kr_out, q_out,
    wq, wk, wv, lp, rr, qg, wvt, trig, ssem, rsem, lsem,
):
    seq = lax.axis_index("seq")
    tp = lax.axis_index("tp")
    z, c = seq // 2, lax.rem(seq, 2)
    x, y = tp // NY, lax.rem(tp, NY)
    oc = 1 - c

    def zmod(d):
        return lax.rem(z + (d + NZ), NZ)

    def col(dx, dy):
        return (x if dx == 0 else 1 - x) * NY + lax.rem(y + (dy + NY), NY)

    right = {"seq": zmod(1) * 2 + c}
    left = {"seq": zmod(-1) * 2 + c}
    sibling = {"seq": z * 2 + oc}
    xside = {"tp": col(1, 0)}
    yup = {"tp": col(0, 1)}
    ydown = {"tp": col(0, -1)}
    offs = (0, -1, 1, -2, 2, -3, 3, 4)

    local = [
        pltpu.make_async_copy(query_hbm.at[0], qg.at[tp], lsem.at[0]),
        pltpu.make_async_copy(uk_hbm, wk.at[seq], lsem.at[1]),
        pltpu.make_async_copy(uv_hbm, wv.at[seq], lsem.at[2]),
        pltpu.make_async_copy(uq_hbm, wq.at[seq], lsem.at[3]),
    ]
    for cp in local:
        cp.start()
    barrier = pltpu.get_barrier_semaphore()
    for peer in (right, left, sibling, xside, yup, ydown):
        pl.semaphore_signal(barrier, inc=1, device_id=peer, device_id_type=MESH)

    lp[tp, c, 0] = folded(key_ref[0])
    lane = lax.broadcasted_iota(jnp.int32, (BLK, 2 * ROPE), 1)
    row = lax.broadcasted_iota(jnp.int32, (BLK, 2 * ROPE), 0)
    p0, p1 = order[0, 2 * seq] * BLK, order[0, 2 * seq + 1] * BLK
    kpos = row + jnp.where(lane < ROPE, p0, p1)
    cosine, sine = turning(kpos, lane)
    raw = folded(rope_ref[0].astype(F32))
    rr[c, z] = (raw * cosine + swapped(raw) * sine).astype(BF16)
    for b, p in ((0, p0), (1, p1)):
        cosine, sine = turning(row + p, lane)
        trig[0, b * BLK : (b + 1) * BLK] = cosine
        trig[1, b * BLK : (b + 1) * BLK] = sine

    sends = []
    names = {}

    def sem_of(key):
        if key not in names:
            names[key] = len(names)
        return rsem.at[names[key]]

    def send(src, dst, key, peer):
        cp = pltpu.make_async_remote_copy(
            src_ref=src, dst_ref=dst, send_sem=ssem.at[len(sends)], recv_sem=sem_of(key),
            device_id=peer, device_id_type=MESH,
        )
        cp.start()
        sends.append(cp)

    def arrived(ref, key):
        pltpu.make_async_remote_copy(
            src_ref=ref, dst_ref=ref, send_sem=ssem.at[0], recv_sem=sem_of(key),
            device_id=sibling, device_id_type=MESH,
        ).wait_recv()

    half = wq.shape[1] // 2

    def piece(item, sid, core):
        zs = zmod(offs[sid])
        if item == "l":
            return lp.at[tp, core, sid]
        if item == "r":
            return rr.at[core, zs]
        if item == "k":
            return wk.at[zs * 2 + core]
        if item == "v":
            return wv.at[zs * 2 + core]
        return wq.at[zs * 2 + core, pl.ds(half * int(item[1]), half)]

    def moved(item, sid, going):
        if item == "l":
            nxt = {0: 1, 1: 3, 3: 5, 5: 7} if going == "r" else {0: 2, 2: 4, 4: 6, 6: 7}
            return lp.at[tp, c, nxt[sid]], nxt[sid]
        nxt = {0: 1, 1: 3, 3: 5, 5: 7} if going == "r" else {0: 2, 2: 4, 4: 6, 6: 7}
        return piece(item, sid, c), nxt[sid]

    by_right = ("l", "r", "k", "q0")

    def pass_on(item, sid):
        src = piece(item, sid, c)
        if sid in (0, 1, 3) or (sid == 5 and item in by_right):
            dst, n = moved(item, sid, "r")
            send(src, dst, ("ring", item, n), right)
        if sid in (0, 2, 4) or (sid == 6 and item not in by_right):
            dst, n = moved(item, sid, "l")
            send(src, dst, ("ring", item, n), left)
        send(src, src, ("sib", item, sid), sibling)

    def ring(item, *sids):
        for sid in sids:
            arrived(piece(item, sid, c), ("ring", item, sid))
            pass_on(item, sid)

    def part(item, column, core=None):
        if item == "Q":
            return qg.at[column]
        return lp.at[column, c if core is None else core, pl.ds(2 * item, 2)]

    def share(item, column, name):
        if item != "Q":
            ref = part(item, column)
            send(ref, ref, ("share", item, name), sibling)

    def plane_own(item):
        ref = part(item, tp)
        send(ref, ref, ("x", item), xside)
        send(ref, ref, ("up", item, 0), yup)
        send(ref, ref, ("down", item, 0), ydown)

    def plane_x(item):
        ref = part(item, col(1, 0))
        arrived(ref, ("x", item))
        send(ref, ref, ("up", item, 1), yup)
        send(ref, ref, ("down", item, 1), ydown)
        share(item, col(1, 0), "x")

    def plane_y(item):
        for k in (0, 1):
            ref = part(item, col(k, -1))
            arrived(ref, ("up", item, k))
            if k == 0:
                send(ref, ref, ("far", item, 0), yup)
            share(item, col(k, -1), ("up", k))
            ref = part(item, col(k, 1))
            arrived(ref, ("down", item, k))
            if k == 1:
                send(ref, ref, ("far", item, 1), ydown)
            share(item, col(k, 1), ("down", k))

    def plane_far(item):
        for k in (0, 1):
            arrived(part(item, col(k, 2)), ("far", item, k))
            share(item, col(k, 2), ("far", k))

    def from_sibling(item):
        for sid in range(NZ):
            arrived(piece(item, sid, oc), ("sib", item, sid))

    def shared(item):
        arrived(part(item, col(1, 0), oc), ("share", item, "x"))
        for k in (0, 1):
            arrived(part(item, col(k, -1), oc), ("share", item, ("up", k)))
            arrived(part(item, col(k, 1), oc), ("share", item, ("down", k)))
            arrived(part(item, col(k, 2), oc), ("share", item, ("far", k)))

    def project(group):
        def one(i, carry):
            core = i // 2
            sid = 2 * group + lax.rem(i, 2)
            d = (sid + 1) // 2
            away = jnp.where(lax.rem(sid, 2) == 0, d, NZ - d)
            zs = lax.rem(z + away, NZ)
            low, high = [], []
            for pair in range(NTP // 2):
                a, b = lp[2 * pair, core, sid], lp[2 * pair + 1, core, sid]
                low.append(jnp.concatenate([a[:, :64], b[:, :64]], axis=1))
                high.append(jnp.concatenate([a[:, 64:], b[:, 64:]], axis=1))
            latent = jnp.concatenate(
                [jnp.concatenate(low, axis=1), jnp.concatenate(high, axis=1)], axis=0
            )
            first = pl.multiple_of((zs * 2 + core) * 256, 256)
            weight = wk[...].reshape(-1, wk.shape[2])
            k_out[pl.ds(first, 256), :] = jnp.dot(
                latent, weight, preferred_element_type=F32
            ).astype(BF16)
            vt_out[:, pl.ds(first, 256)] = lax.dot_general(
                wvt[...], latent, (((1,), (1,)), ((), ())), preferred_element_type=F32
            ).astype(BF16)
            rot = rr[core, zs]
            kr_out[pl.ds(first, BLK), :] = jnp.concatenate([rot[:, :64], rot[:, :64]], axis=1)
            kr_out[pl.ds(first + BLK, BLK), :] = jnp.concatenate([rot[:, 64:], rot[:, 64:]], axis=1)
            return carry

        lax.fori_loop(0, 4, one, 0)

    pl.semaphore_wait(barrier, 6)
    for item in ("l", "r"):
        pass_on(item, 0)
    local[0].wait()
    plane_own("Q")
    local[1].wait()
    local[2].wait()
    for item in ("k", "v"):
        pass_on(item, 0)
    local[3].wait()
    ring("l", 1, 2)
    ring("r", 1, 2)
    plane_own(0)
    plane_x("Q")
    ring("k", 1, 2)
    ring("v", 1, 2)
    for item in ("q0", "q1"):
        pass_on(item, 0)
    ring("l", 3, 4)
    ring("r", 3, 4)
    plane_own(1)
    plane_x(0)
    plane_y("Q")
    ring("k", 3, 4)
    ring("v", 3, 4)
    ring("l", 5, 6)
    ring("r", 5, 6)
    plane_own(2)
    plane_x(1)
    ring("q0", 1, 2)
    ring("q1", 1, 2)
    plane_y(0)
    ring("l", 7)
    ring("r", 7)
    plane_own(3)
    plane_x(2)
    plane_far("Q")
    ring("k", 5, 6)
    ring("v", 5, 6)
    plane_y(1)
    plane_far(0)
    plane_x(3)
    ring("k", 7)
    ring("v", 7)
    ring("q0", 3, 4)
    ring("q1", 3, 4)
    plane_y(2)
    plane_far(1)
    for item in ("l", "r", "k", "v"):
        from_sibling(item)
    wvt[...] = wv[...].reshape(-1, wv.shape[2]).astype(F32).T.astype(BF16)
    shared(0)
    project(0)
    plane_y(3)
    plane_far(2)
    ring("q0", 5, 6)
    ring("q1", 5, 6)
    shared(1)
    project(1)
    plane_far(3)
    shared(2)
    project(2)
    ring("q0", 7)
    ring("q1", 7)
    shared(3)
    project(3)
    from_sibling("q0")
    from_sibling("q1")

    rows_q = wq.shape[1] * 2

    def heads_pair(pair, carry):
        cols = pl.ds(pl.multiple_of(pair * 384, 128), 384)
        acc = jnp.zeros((256, 384), F32)
        for t in range(NTP):
            acc = acc + jnp.dot(
                qg[t],
                wq[2 * t : 2 * t + 2, :, cols].reshape(rows_q, 384),
                preferred_element_type=F32,
            )
        t0, t1, t2 = acc[:, :128], acc[:, 128:256], acc[:, 256:]
        at = lax.broadcasted_iota(jnp.int32, (256, 128), 1)
        rope = jnp.where(at < ROPE, t1, t2)
        rope = rope * trig[0] + swapped(rope) * trig[1]
        nope1 = jnp.concatenate([t1[:, 64:], t2[:, :64]], axis=1)
        q_out[2 * pair, :, :128] = t0.astype(BF16)
        q_out[2 * pair, :, 128:] = jnp.where(at < ROPE, rope, 0.0).astype(BF16)
        q_out[2 * pair + 1, :, :128] = nope1.astype(BF16)
        q_out[2 * pair + 1, :, 128:] = jnp.where(at < ROPE, 0.0, rope).astype(BF16)
        return carry

    lax.fori_loop(0, 4, heads_pair, 0)
    for cp in sends:
        cp.wait_send()


def attention_kernel(order, segs, seg_rows, q_ref, k_ref, vt_ref, kr_ref, out_ref, max_ref, inv, acc, m_ref, l_ref):
    heads = q_ref.shape[0]
    blocks = order.shape[1]
    seq = lax.axis_index("seq")
    scale = 1.0 / math.sqrt(NOPE + ROPE)

    def note(i, carry):
        inv[order[0, i]] = i
        return carry

    lax.fori_loop(0, blocks, note, 0)
    seg = seg_rows[...]
    starts = [jnp.sum((seg < v).astype(jnp.int32)) for v in (1, 2, 3)]

    def start_of(label):
        return jnp.where(
            label == 0, 0, jnp.where(label == 1, starts[0], jnp.where(label == 2, starts[1], starts[2]))
        )

    for qb in range(2):
        p = order[0, 2 * seq + qb]
        begin = start_of(segs[0, p * BLK])
        low = begin // BLK
        count = (p - low + 2) // 2
        label_row = seg_rows[pl.ds(p, 1), :]
        start_row = start_of(label_row)
        qpos = lax.broadcasted_iota(jnp.int32, (1, BLK), 1) + p * BLK
        m_ref[...] = jnp.full_like(m_ref, masked_value)
        l_ref[...] = jnp.zeros_like(l_ref)
        acc[...] = jnp.zeros_like(acc)

        def step(i, carry):
            ja = p - 2 * i
            jb = ja - 1
            ra = pl.multiple_of(inv[ja] * BLK, BLK)
            rb = pl.multiple_of(inv[jnp.maximum(jb, 0)] * BLK, BLK)
            kin = lax.broadcasted_iota(jnp.int32, (BLK, BLK), 0)
            kpos = jnp.concatenate([kin + ja * BLK, kin + jb * BLK], axis=0)
            bias = jnp.where((kpos >= start_row) & (kpos <= qpos), 0.0, masked_value)
            kr = jnp.concatenate([kr_ref[pl.ds(ra, BLK), :], kr_ref[pl.ds(rb, BLK), :]], axis=0)
            for h in range(heads):
                cols = slice(h * 128, (h + 1) * 128)
                kn = jnp.concatenate(
                    [k_ref[pl.ds(ra, BLK), cols], k_ref[pl.ds(rb, BLK), cols]], axis=0
                )
                s = lax.dot_general(
                    jnp.concatenate([kn, kr], axis=1),
                    q_ref[h, qb * BLK : (qb + 1) * BLK, :],
                    (((1,), (1,)), ((), ())),
                    preferred_element_type=F32,
                )
                s = s * scale + bias
                old = m_ref[h : h + 1, :]
                new = jnp.maximum(old, jnp.max(s, axis=0, keepdims=True))
                w = jnp.exp(s - new)
                shrink = jnp.exp(old - new)
                m_ref[h : h + 1, :] = new
                l_ref[h : h + 1, :] = l_ref[h : h + 1, :] * shrink + jnp.sum(w, axis=0, keepdims=True)
                vt = jnp.concatenate(
                    [vt_ref[cols, pl.ds(ra, BLK)], vt_ref[cols, pl.ds(rb, BLK)]], axis=1
                )
                acc[h] = acc[h] * shrink + jnp.dot(vt, w.astype(BF16), preferred_element_type=F32)
            return carry

        lax.fori_loop(0, count, step, 0)
        for h in range(heads):
            out_ref[0, qb * BLK : (qb + 1) * BLK, h * VD : (h + 1) * VD] = (
                (acc[h] / l_ref[h : h + 1, :]).T.astype(BF16)
            )
        if qb == 0:
            max_ref[...] = m_ref[...]
        else:
            max_ref[...] = jnp.maximum(max_ref[...], m_ref[...])


def exchange_kernel(nseq, ndp, max_ref, out_ref, mine, got, ssem, rsem, lsem):
    seq, dp = lax.axis_index("seq"), lax.axis_index("dp")
    own = pltpu.make_async_copy(max_ref, mine, lsem.at[0])
    own.start()
    barrier = pltpu.get_barrier_semaphore()
    peers = []
    for n in range(1, nseq * ndp):
        ds, dd = n % nseq, n // nseq
        peers.append({"seq": lax.rem(seq + ds, nseq), "dp": lax.rem(dp + dd, ndp)})
    for peer in peers:
        pl.semaphore_signal(barrier, inc=1, device_id=peer, device_id_type=MESH)
    own.wait()
    pl.semaphore_wait(barrier, len(peers))
    sends = []
    for n, peer in enumerate(peers):
        cp = pltpu.make_async_remote_copy(
            src_ref=mine, dst_ref=got.at[n], send_sem=ssem.at[n], recv_sem=rsem.at[n],
            device_id=peer, device_id_type=MESH,
        )
        cp.start()
        sends.append(cp)
    best = mine[...]
    for n, cp in enumerate(sends):
        cp.wait_recv()
        best = jnp.maximum(best, got[n])
    out_ref[...] = best
    for cp in sends:
        cp.wait_send()


def on_device(nseq, ndp, query_latent, key_latent, rope_key, w_uq, w_uk, w_uv, block_order, segment_ids):
    heads = w_uq.shape[1] // (NOPE + ROPE)
    tokens = key_latent.shape[1]
    total = tokens * nseq
    vmem, anyw, smem = (
        pl.BlockSpec(memory_space=pltpu.VMEM),
        pl.BlockSpec(memory_space=pl.ANY),
        pl.BlockSpec(memory_space=pltpu.SMEM),
    )
    k_all, vt_all, kr_all, q_all = pl.pallas_call(
        gather_kernel,
        out_shape=(
            pltpu.VMEM((total, heads * NOPE), BF16),
            pltpu.VMEM((heads * VD, total), BF16),
            pltpu.VMEM((total, 2 * ROPE), BF16),
            pltpu.VMEM((heads, tokens, 256), BF16),
        ),
        in_specs=[smem, vmem, vmem, anyw, anyw, anyw, anyw],
        out_specs=(vmem, vmem, vmem, vmem),
        scratch_shapes=[
            pltpu.VMEM((nseq, *w_uq.shape), BF16),
            pltpu.VMEM((nseq, *w_uk.shape), BF16),
            pltpu.VMEM((nseq, *w_uv.shape), BF16),
            pltpu.VMEM((NTP, 2, NZ, BLK, 2 * key_latent.shape[2]), BF16),
            pltpu.VMEM((2, NZ, BLK, 2 * ROPE), BF16),
            pltpu.VMEM((NTP, tokens, query_latent.shape[2]), BF16),
            pltpu.VMEM((w_uv.shape[1], nseq * w_uv.shape[0]), BF16),
            pltpu.VMEM((2, tokens, 2 * ROPE), F32),
            pltpu.SemaphoreType.DMA((160,)),
            pltpu.SemaphoreType.DMA((160,)),
            pltpu.SemaphoreType.DMA((4,)),
        ],
        compiler_params=pltpu.CompilerParams(
            collective_id=0, has_side_effects=True, vmem_limit_bytes=40 * MIB
        ),
        name="gather",
    )(block_order, rope_key, key_latent, query_latent, w_uq, w_uk, w_uv)
    context, row_max = pl.pallas_call(
        attention_kernel,
        out_shape=(
            jax.ShapeDtypeStruct((1, tokens, heads * VD), BF16),
            jax.ShapeDtypeStruct((heads, BLK), F32),
        ),
        in_specs=[smem, smem, vmem, vmem, vmem, vmem, vmem],
        out_specs=(vmem, vmem),
        scratch_shapes=[
            pltpu.SMEM((block_order.shape[1],), jnp.int32),
            pltpu.VMEM((heads, VD, BLK), F32),
            pltpu.VMEM((heads, BLK), F32),
            pltpu.VMEM((heads, BLK), F32),
        ],
        compiler_params=pltpu.CompilerParams(vmem_limit_bytes=32 * MIB),
        name="attend",
    )(
        block_order, segment_ids, segment_ids.reshape(-1, BLK),
        q_all, k_all, vt_all, kr_all,
    )
    n = nseq * ndp - 1
    best = pl.pallas_call(
        functools.partial(exchange_kernel, nseq, ndp),
        out_shape=jax.ShapeDtypeStruct((heads, BLK), F32),
        in_specs=[anyw],
        out_specs=vmem,
        scratch_shapes=[
            pltpu.VMEM((heads, BLK), F32),
            pltpu.VMEM((n, heads, BLK), F32),
            pltpu.SemaphoreType.DMA((n,)),
            pltpu.SemaphoreType.DMA((n,)),
            pltpu.SemaphoreType.DMA((1,)),
        ],
        compiler_params=pltpu.CompilerParams(collective_id=1, has_side_effects=True),
        name="exchange",
    )(row_max)
    head_max = jnp.max(best, axis=1)
    ratio = CLIP / jnp.maximum(head_max, CLIP)
    root = jnp.sqrt(ratio)
    factors = jnp.concatenate(
        [
            jnp.broadcast_to(root[:, None], (heads, NOPE)),
            jnp.broadcast_to(ratio[:, None], (heads, ROPE)),
        ],
        axis=1,
    ).reshape(heads * (NOPE + ROPE))
    clipped_uq = (w_uq.astype(F32) * factors[None, :]).astype(BF16)
    clipped_uk = (w_uk.astype(F32) * jnp.repeat(root, NOPE)[None, :]).astype(BF16)
    return (context, clipped_uq, clipped_uk)


def solution(mesh):
    placed = (
        P("dp", "seq", "tp"),
        P("dp", "seq", "tp"),
        P("dp", "seq", None),
        P("seq", "tp"),
        P("seq", "tp"),
        P("seq", "tp"),
        P("dp", None),
        P("dp", None),
    )
    return jax.shard_map(
        functools.partial(on_device, mesh.shape["seq"], mesh.shape["dp"]),
        mesh=mesh,
        in_specs=placed,
        out_specs=(P("dp", "seq", "tp"), P("seq", "tp"), P("seq", "tp")),
        check_vma=False,
    )
```

time: 320 us -> 130 us (0.41)
  Pallas kernels: 0 us -> 109 us
  waiting for transfers between devices: 84.9 us -> 0 us
  matrix products: 80.3 us -> 0 us
  blocking collectives: 48.7 us -> 0 us
  other arithmetic: 34.6 us -> 2.22 us
  local copies, waits for them, and re-layouts: 43.6 us -> 20.1 us
  between operations: 13.9 us -> 0.67 us
  starting transfers between devices: 6.74 us -> 0 us
  loops' own time: 6.11 us -> 0 us
    pallas_call x0 -> x3, Pallas kernels: none -> 109 us  [the longest x1 61 us: on_device(): pl.pallas_call(gather_kernel, out_shape=(pltpu.VMEM((total, heads * NOPE)...]
    dot_general x41 -> x0, matrix products: 80.3 us -> none  [the longest x8 23.8 us: block_step(): jnp.einsum('hqr,kr->hqk', query_rope, rope_block, preferred_element_type=...]
    all_gather x3 -> x0, waiting for transfers between devices: 76.6 us -> none  [the longest x2 46.1 us: in_one_piece(): lax.all_gather(both, axis, axis=dim, tiled=True)]
    all_gather x2 -> x0, blocking collectives: 48.7 us -> none  [the longest x1 24.7 us: on_device(): lax.all_gather(query_latent[0], 'tp', axis=1, tiled=True)]
    gather x9 -> x0, local copies, waits for them, and re-layouts: 27.1 us -> none  [the longest x8 25.1 us: block_step(): key_labels = jnp.take(labels_all, key_pos)]
    reduce_sum x17 -> x0, other arithmetic: 26 us -> none  [the longest x8 24.5 us: block_step(): new_total = run_total * shrink + jnp.sum(weights, axis=2)]
    unnamed x11 -> x21, local copies, waits for them, and re-layouts: 1.46 us -> 19.8 us
    slice x4 -> x0, local copies, waits for them, and re-layouts: 7.94 us -> none  [in_one_piece(): lax.slice_in_dim(whole, at, at + a.shape[along], axis=along)]
  transfers between devices with their start and end apart: 4 -> 0, of which waited for: 3 -> 0; matrix products, arithmetic and copies ran while one was open for 5% -> 0% of each run, Pallas kernels for 0% -> 0%
where the time goes in v1:
time: 130 us; the launch traced here: 132 us
  Pallas kernels  109 us (84%)
  local copies, waits for them, and re-layouts  20.1 us (15%)
  other arithmetic  2.22 us (2%)
    pallas_call x1, Pallas kernels, on_device(): pl.pallas_call(gather_kernel, out_shape=(pltpu.VMEM((total, heads * NOPE)...  61 us
    pallas_call x1, Pallas kernels, on_device(): pl.pallas_call(attention_kernel, out_shape=(jax.ShapeDtypeStruct((1, toke...  25.4 us
    pallas_call x1, Pallas kernels, on_device(): pl.pallas_call(functools.partial(exchange_kernel, nseq, ndp), out_shape=j...  22.2 us
    unnamed x21, local copies, waits for them, and re-layouts  19.8 us

profile of v1, /device:TPU:1, one launch (start us, length us, event | category | flops | bytes accessed | tf_op | source)
XLA Modules:
  0.0 131.7 jit_solution(5071505693922671281)
XLA Ops:
  0.6 1.5 %copy.12.key_ref = bf16[1,256,64]{2,1,0:T(8,128)(2,1)} copy(bf16[1,256,64]{1,2,0:T(8,128)(2,1)} %param.9) | data formatting | bytes 65536 | tf_op args[1]
  2.1 1.5 %copy.11.rope_ref = bf16[1,256,64]{2,1,0:T(8,128)(2,1)} copy(bf16[1,256,64]{1,2,0:T(8,128)(2,1)} %param.10) | data formatting | bytes 65536 | tf_op args[2]
  3.6 1.7 %copy.13.query_hbm = bf16[1,256,192]{2,1,0:T(8,128)(2,1)} copy(bf16[1,256,192]{1,2,0:T(8,128)(2,1)} %param.8) | data formatting | bytes 196608 | tf_op args[0]
  5.3 61.0 %gather.1 = (bf16[4096,1024]{1,0:T(8,128)(2,1)S(1)}, bf16[1024,4096]{1,0:T(8,128)(2,1)S(1)}, bf16[4096,128]{1,0:T(8,128)(2,1)S(1)}, bf16[8,256,256]{2,1,0:T(8,128)(2,1)S(1)}) custom-call(s32[1,32]{1,0:T(1,128)} %order.3, bf16[1,256,64]{2,1,0:T(8,128)(2,1)} %copy.11.rope_ref, bf16[1,256,64]{2,1,0:T(8,128)(2,1)} %copy.12.key_ref, ...), custom_call_target="tpu_custom_call" | custom-call | tf_op jit(solution)/shard_map/gather/pallas_call | solution.py:472
  66.3 0.0 copy-start
  66.3 3.2 %copy-done = bf16[4096,1024]{1,0:T(8,128)(2,1)} copy-done((bf16[4096,1024]{1,0:T(8,128)(2,1)}, bf16[4096,1024]{1,0:T(8,128)(2,1)S(1)}, u32[]{:S(2)}) %copy-start) | copy-done | bytes 8388632
  69.5 0.0 copy-start.2
  69.5 3.2 %copy-done.2 = bf16[1024,4096]{1,0:T(8,128)(2,1)} copy-done((bf16[1024,4096]{1,0:T(8,128)(2,1)}, bf16[1024,4096]{1,0:T(8,128)(2,1)S(1)}, u32[]{:S(2)}) %copy-start.2) | copy-done | bytes 8388632
  72.7 0.0 copy-start.1
  72.8 3.4 %copy-done.1 = bf16[4096,1024]{1,0:T(8,128)(2,1)S(1)} copy-done((bf16[4096,1024]{1,0:T(8,128)(2,1)S(1)}, bf16[4096,1024]{1,0:T(8,128)(2,1)}, u32[]{:S(2)}) %copy-start.1) | copy-done | bytes 8388632
  76.1 0.0 copy-start.3
  76.1 3.4 %copy-done.3 = bf16[1024,4096]{1,0:T(8,128)(2,1)S(1)} copy-done((bf16[1024,4096]{1,0:T(8,128)(2,1)S(1)}, bf16[1024,4096]{1,0:T(8,128)(2,1)}, u32[]{:S(2)}) %copy-start.3) | copy-done | bytes 8388632
  79.5 0.0 copy-start.4
  79.5 0.7 copy-done.4
  80.2 0.0 copy-start.6
  80.2 0.7 copy-done.6
  80.9 0.0 copy-start.8
  80.9 0.0 copy-start.7
  80.9 25.4 %attend.1 = (bf16[1,256,1024]{2,1,0:T(8,128)(2,1)}, f32[8,128]{1,0:T(8,128)S(1)}) custom-call(s32[1,32]{1,0:T(1,128)S(1)} %copy-done.6, s32[1,4096]{1,0:T(1,128)S(1)} %copy-done.4, s32[32,128]{1,0:T(8,128)S(1)} %bitcast.3, bf16[8,256,256]{2,1,0:T(8,128)(2,1)S(1)} %get-tuple-element.9.q_ref, bf16[4096,1024]{1,0:T(8,128)(2,1)S(1)} %copy-done.1, ...), custom_call_target="tpu_custom_call" | custom-call | tf_op jit(solution)/shard_map/attend/pallas_call | solution.py:500
  106.3 0.0 copy-start.5
  106.3 0.6 copy-done.5
  106.9 22.2 %exchange.1 = f32[8,128]{1,0:T(8,128)} custom-call(f32[8,128]{1,0:T(8,128)} %copy-done.5), custom_call_target="tpu_custom_call" | custom-call | tf_op jit(solution)/shard_map/exchange/pallas_call | solution.py:521
  129.1 0.8 reduce_max.9
  129.9 0.1 broadcast_in_dim.5
  130.0 0.1 broadcast_bitcast_fusion
  130.1 0.1 broadcast_in_dim.4
  130.2 0.1 mul.20
  130.2 0.0 copy-done.8
  130.2 0.7 multiply_convert_fusion.1
  130.9 0.0 copy-done.7
  130.9 0.8 multiply_convert_fusion
  (2 shorter events, 0.0 us)
Async XLA Ops:
  66.3 3.2 %copy-start = (bf16[4096,1024]{1,0:T(8,128)(2,1)}, bf16[4096,1024]{1,0:T(8,128)(2,1)S(1)}, u32[]{:S(2)}) copy-start(bf16[4096,1024]{1,0:T(8,128)(2,1)S(1)} %get-tuple-element.10.k_ref) | copy-start | bytes 25165828
  69.5 3.2 %copy-start.2 = (bf16[1024,4096]{1,0:T(8,128)(2,1)}, bf16[1024,4096]{1,0:T(8,128)(2,1)S(1)}, u32[]{:S(2)}) copy-start(bf16[1024,4096]{1,0:T(8,128)(2,1)S(1)} %get-tuple-element.11.vt_ref) | copy-start | bytes 25165828
  72.7 3.4 %copy-start.1 = (bf16[4096,1024]{1,0:T(8,128)(2,1)S(1)}, bf16[4096,1024]{1,0:T(8,128)(2,1)}, u32[]{:S(2)}) copy-start(bf16[4096,1024]{1,0:T(8,128)(2,1)} %copy-done) | copy-start | bytes 25165828
  76.1 3.4 %copy-start.3 = (bf16[1024,4096]{1,0:T(8,128)(2,1)S(1)}, bf16[1024,4096]{1,0:T(8,128)(2,1)}, u32[]{:S(2)}) copy-start(bf16[1024,4096]{1,0:T(8,128)(2,1)} %copy-done.2) | copy-start | bytes 25165828
  79.5 0.7 copy-start.4
  80.2 0.7 copy-start.6
  80.9 49.4 %copy-start.8 = (bf16[32,1024]{1,0:T(8,128)(2,1)S(1)}, bf16[32,1024]{1,0:T(8,128)(2,1)}, u32[]{:S(2)}) copy-start(bf16[32,1024]{1,0:T(8,128)(2,1)} %uk_hbm.1) | copy-start | bytes 196612
  80.9 50.0 %copy-start.7 = (bf16[96,1536]{1,0:T(8,128)(2,1)S(1)}, bf16[96,1536]{1,0:T(8,128)(2,1)}, u32[]{:S(2)}) copy-start(bf16[96,1536]{1,0:T(8,128)(2,1)} %uq_hbm.1) | copy-start | bytes 884740
  106.3 0.6 copy-start.5

commit v2 on v1

--- a/solution.py
+++ b/solution.py
@@ -17,6 +17,7 @@
 NX = 2
 NTP = NX * NY
 BLK = 128
+RUN = 4
 MIB = 1 << 20
 
 rope_base = 50000.0
@@ -47,28 +48,18 @@
     return cosine, sine
 
 
-def turning(pos, lane):
-    step = lax.rem(lane, ROPE // 2).astype(F32) * (2.0 / ROPE)
-    freq = jnp.exp(-math.log(rope_base) * step)
-    cosine, sine = cos_sin(pos.astype(F32) * freq)
-    sine = jnp.where(lax.rem(lane, ROPE) < ROPE // 2, -sine, sine)
-    return cosine, sine
-
-
-def swapped(x):
-    h = ROPE // 2
-    return jnp.concatenate(
-        [x[:, h : 2 * h], x[:, :h], x[:, 3 * h : 4 * h], x[:, 2 * h : 3 * h]], axis=1
-    )
-
-
-def folded(x):
-    n = x.shape[0] // 2
-    return jnp.concatenate([x[:n], x[n:]], axis=1)
+def turning(pos):
+    step = lax.broadcasted_iota(jnp.int32, pos.shape, 0).astype(F32) * (2.0 / ROPE)
+    return cos_sin(pos.astype(F32) * jnp.exp(-math.log(rope_base) * step))
+
+
+def rotated(x, cosine, sine):
+    a, b = x[: ROPE // 2], x[ROPE // 2 :]
+    return jnp.concatenate([a * cosine - b * sine, b * cosine + a * sine], axis=0)
 
 
 def gather_kernel(
-    order, rope_ref, key_ref, query_hbm, uq_hbm, uk_hbm, uv_hbm,
+    order, rope_ref, key_hbm, query_hbm, uq_hbm, uk_hbm, uv_hbm,
     k_out, vt_out, kr_out, q_out,
     wq, wk, wv, lp, rr, qg, wvt, trig, ssem, rsem, lsem,
 ):
@@ -93,6 +84,7 @@
     offs = (0, -1, 1, -2, 2, -3, 3, 4)
 
     local = [
+        pltpu.make_async_copy(key_hbm.at[0], lp.at[tp, c, 0], lsem.at[4]),
         pltpu.make_async_copy(query_hbm.at[0], qg.at[tp], lsem.at[0]),
         pltpu.make_async_copy(uk_hbm, wk.at[seq], lsem.at[1]),
         pltpu.make_async_copy(uv_hbm, wv.at[seq], lsem.at[2]),
@@ -104,18 +96,12 @@
     for peer in (right, left, sibling, xside, yup, ydown):
         pl.semaphore_signal(barrier, inc=1, device_id=peer, device_id_type=MESH)
 
-    lp[tp, c, 0] = folded(key_ref[0])
-    lane = lax.broadcasted_iota(jnp.int32, (BLK, 2 * ROPE), 1)
-    row = lax.broadcasted_iota(jnp.int32, (BLK, 2 * ROPE), 0)
+    lane = lax.broadcasted_iota(jnp.int32, (ROPE // 2, 2 * BLK), 1)
     p0, p1 = order[0, 2 * seq] * BLK, order[0, 2 * seq + 1] * BLK
-    kpos = row + jnp.where(lane < ROPE, p0, p1)
-    cosine, sine = turning(kpos, lane)
-    raw = folded(rope_ref[0].astype(F32))
-    rr[c, z] = (raw * cosine + swapped(raw) * sine).astype(BF16)
-    for b, p in ((0, p0), (1, p1)):
-        cosine, sine = turning(row + p, lane)
-        trig[0, b * BLK : (b + 1) * BLK] = cosine
-        trig[1, b * BLK : (b + 1) * BLK] = sine
+    cosine, sine = turning(jnp.where(lane < BLK, p0 + lane, p1 + (lane - BLK)))
+    trig[0] = cosine
+    trig[1] = sine
+    rr[c, z] = rotated(rope_ref[0].astype(F32), cosine, sine).astype(BF16)
 
     sends = []
     names = {}
@@ -236,39 +222,32 @@
             d = (sid + 1) // 2
             away = jnp.where(lax.rem(sid, 2) == 0, d, NZ - d)
             zs = lax.rem(z + away, NZ)
-            low, high = [], []
-            for pair in range(NTP // 2):
-                a, b = lp[2 * pair, core, sid], lp[2 * pair + 1, core, sid]
-                low.append(jnp.concatenate([a[:, :64], b[:, :64]], axis=1))
-                high.append(jnp.concatenate([a[:, 64:], b[:, 64:]], axis=1))
-            latent = jnp.concatenate(
-                [jnp.concatenate(low, axis=1), jnp.concatenate(high, axis=1)], axis=0
-            )
+            latent = lp[:, core, sid].reshape(-1, 256)
             first = pl.multiple_of((zs * 2 + core) * 256, 256)
             weight = wk[...].reshape(-1, wk.shape[2])
-            k_out[pl.ds(first, 256), :] = jnp.dot(
-                latent, weight, preferred_element_type=F32
+            k_out[pl.ds(first, 256), :] = lax.dot_general(
+                latent, weight, (((0,), (0,)), ((), ())), preferred_element_type=F32
             ).astype(BF16)
-            vt_out[:, pl.ds(first, 256)] = lax.dot_general(
-                wvt[...], latent, (((1,), (1,)), ((), ())), preferred_element_type=F32
+            vt_out[:, pl.ds(first, 256)] = jnp.dot(
+                wvt[...], latent, preferred_element_type=F32
             ).astype(BF16)
-            rot = rr[core, zs]
-            kr_out[pl.ds(first, BLK), :] = jnp.concatenate([rot[:, :64], rot[:, :64]], axis=1)
-            kr_out[pl.ds(first + BLK, BLK), :] = jnp.concatenate([rot[:, 64:], rot[:, 64:]], axis=1)
+            rot = rr[core, zs].astype(F32)
+            kr_out[pl.ds(first, 256), :] = jnp.concatenate([rot, jnp.zeros_like(rot)], axis=0).T.astype(BF16)
             return carry
 
         lax.fori_loop(0, 4, one, 0)
 
     pl.semaphore_wait(barrier, 6)
+    local[0].wait()
     for item in ("l", "r"):
         pass_on(item, 0)
-    local[0].wait()
+    local[1].wait()
     plane_own("Q")
-    local[1].wait()
     local[2].wait()
+    local[3].wait()
     for item in ("k", "v"):
         pass_on(item, 0)
-    local[3].wait()
+    local[4].wait()
     ring("l", 1, 2)
     ring("r", 1, 2)
     plane_own(0)
@@ -328,26 +307,18 @@
     from_sibling("q0")
     from_sibling("q1")
 
-    rows_q = wq.shape[1] * 2
+    query = qg[...].reshape(-1, 256)
 
     def heads_pair(pair, carry):
         cols = pl.ds(pl.multiple_of(pair * 384, 128), 384)
-        acc = jnp.zeros((256, 384), F32)
-        for t in range(NTP):
-            acc = acc + jnp.dot(
-                qg[t],
-                wq[2 * t : 2 * t + 2, :, cols].reshape(rows_q, 384),
-                preferred_element_type=F32,
-            )
-        t0, t1, t2 = acc[:, :128], acc[:, 128:256], acc[:, 256:]
-        at = lax.broadcasted_iota(jnp.int32, (256, 128), 1)
-        rope = jnp.where(at < ROPE, t1, t2)
-        rope = rope * trig[0] + swapped(rope) * trig[1]
-        nope1 = jnp.concatenate([t1[:, 64:], t2[:, :64]], axis=1)
-        q_out[2 * pair, :, :128] = t0.astype(BF16)
-        q_out[2 * pair, :, 128:] = jnp.where(at < ROPE, rope, 0.0).astype(BF16)
-        q_out[2 * pair + 1, :, :128] = nope1.astype(BF16)
-        q_out[2 * pair + 1, :, 128:] = jnp.where(at < ROPE, 0.0, rope).astype(BF16)
+        acc = lax.dot_general(
+            wq[:, :, cols].reshape(-1, 384), query, (((0,), (0,)), ((), ())), preferred_element_type=F32
+        )
+        for b in (0, 1):
+            one = acc[b * (NOPE + ROPE) : (b + 1) * (NOPE + ROPE)]
+            q_out[2 * pair + b, :NOPE] = one[:NOPE].astype(BF16)
+            q_out[2 * pair + b, NOPE : NOPE + ROPE] = rotated(one[NOPE:], trig[0], trig[1]).astype(BF16)
+            q_out[2 * pair + b, NOPE + ROPE :] = jnp.zeros((ROPE, 256), BF16)
         return carry
 
     lax.fori_loop(0, 4, heads_pair, 0)
@@ -355,14 +326,18 @@
         cp.wait_send()
 
 
-def attention_kernel(order, segs, seg_rows, q_ref, k_ref, vt_ref, kr_ref, out_ref, max_ref, inv, acc, m_ref, l_ref):
-    heads = q_ref.shape[0]
+def attention_kernel(
+    order, segs, seg_rows, q_ref, k_ref, vt_ref, kr_ref, out_ref, max_ref,
+    inv, rows, needed, bias, scores, weights, acc,
+):
+    heads, _, wide = q_ref.shape
     blocks = order.shape[1]
     seq = lax.axis_index("seq")
     scale = 1.0 / math.sqrt(NOPE + ROPE)
+    log2 = scale / math.log(2.0)
 
     def note(i, carry):
-        inv[order[0, i]] = i
+        inv[order[0, i]] = i * BLK
         return carry
 
     lax.fori_loop(0, blocks, note, 0)
@@ -374,60 +349,118 @@
             label == 0, 0, jnp.where(label == 1, starts[0], jnp.where(label == 2, starts[1], starts[2]))
         )
 
-    for qb in range(2):
-        p = order[0, 2 * seq + qb]
-        begin = start_of(segs[0, p * BLK])
-        low = begin // BLK
-        count = (p - low + 2) // 2
-        label_row = seg_rows[pl.ds(p, 1), :]
-        start_row = start_of(label_row)
-        qpos = lax.broadcasted_iota(jnp.int32, (1, BLK), 1) + p * BLK
-        m_ref[...] = jnp.full_like(m_ref, masked_value)
-        l_ref[...] = jnp.zeros_like(l_ref)
-        acc[...] = jnp.zeros_like(acc)
-
-        def step(i, carry):
-            ja = p - 2 * i
-            jb = ja - 1
-            ra = pl.multiple_of(inv[ja] * BLK, BLK)
-            rb = pl.multiple_of(inv[jnp.maximum(jb, 0)] * BLK, BLK)
-            kin = lax.broadcasted_iota(jnp.int32, (BLK, BLK), 0)
-            kpos = jnp.concatenate([kin + ja * BLK, kin + jb * BLK], axis=0)
-            bias = jnp.where((kpos >= start_row) & (kpos <= qpos), 0.0, masked_value)
-            kr = jnp.concatenate([kr_ref[pl.ds(ra, BLK), :], kr_ref[pl.ds(rb, BLK), :]], axis=0)
-            for h in range(heads):
-                cols = slice(h * 128, (h + 1) * 128)
-                kn = jnp.concatenate(
-                    [k_ref[pl.ds(ra, BLK), cols], k_ref[pl.ds(rb, BLK), cols]], axis=0
-                )
-                s = lax.dot_general(
-                    jnp.concatenate([kn, kr], axis=1),
-                    q_ref[h, qb * BLK : (qb + 1) * BLK, :],
-                    (((1,), (1,)), ((), ())),
-                    preferred_element_type=F32,
-                )
-                s = s * scale + bias
-                old = m_ref[h : h + 1, :]
-                new = jnp.maximum(old, jnp.max(s, axis=0, keepdims=True))
-                w = jnp.exp(s - new)
-                shrink = jnp.exp(old - new)
-                m_ref[h : h + 1, :] = new
-                l_ref[h : h + 1, :] = l_ref[h : h + 1, :] * shrink + jnp.sum(w, axis=0, keepdims=True)
-                vt = jnp.concatenate(
-                    [vt_ref[cols, pl.ds(ra, BLK)], vt_ref[cols, pl.ds(rb, BLK)]], axis=1
-                )
-                acc[h] = acc[h] * shrink + jnp.dot(vt, w.astype(BF16), preferred_element_type=F32)
-            return carry
-
-        lax.fori_loop(0, count, step, 0)
-        for h in range(heads):
-            out_ref[0, qb * BLK : (qb + 1) * BLK, h * VD : (h + 1) * VD] = (
-                (acc[h] / l_ref[h : h + 1, :]).T.astype(BF16)
+    p = [order[0, 2 * seq + qb] for qb in (0, 1)]
+    low = [start_of(segs[0, p[qb] * BLK]) // BLK for qb in (0, 1)]
+
+    def choose(j, n):
+        use = ((j >= low[0]) & (j <= p[0])) | ((j >= low[1]) & (j <= p[1]))
+        needed[n] = j
+        rows[n] = inv[j]
+        return n + use.astype(jnp.int32)
+
+    n = lax.fori_loop(0, blocks, choose, 0)
+    for extra in range(RUN - 1):
+        needed[n + extra] = -1
+        rows[n + extra] = 0
+    count = (n + RUN - 1) // RUN
+    start_row = jnp.concatenate([start_of(seg_rows[pl.ds(p[qb], 1), :]) for qb in (0, 1)], axis=1)
+    lanes = lax.broadcasted_iota(jnp.int32, (1, BLK), 1)
+    qpos = jnp.concatenate([lanes + p[0] * BLK, lanes + p[1] * BLK], axis=1)
+
+    def mask(i, carry):
+        inside = lax.broadcasted_iota(jnp.int32, (BLK, wide), 0)
+        for b in range(RUN):
+            kpos = inside + needed[RUN * i + b] * BLK
+            bias[i, b * BLK : (b + 1) * BLK] = jnp.where(
+                (kpos >= start_row) & (kpos <= qpos), 0.0, masked_value
             )
-        if qb == 0:
-            max_ref[...] = m_ref[...]
-        else:
-            max_ref[...] = jnp.maximum(max_ref[...], m_ref[...])
+        return carry
+
+    lax.fori_loop(0, count, mask, 0)
+
+    def spot(i):
+        return [pl.multiple_of(rows[RUN * i + b], BLK) for b in range(RUN)]
+
+    def score(h, i, top):
+        cols = slice(h * NOPE, (h + 1) * NOPE)
+        keys = jnp.concatenate(
+            [
+                jnp.concatenate([k_ref[pl.ds(r, BLK), cols], kr_ref[pl.ds(r, BLK), :]], axis=1)
+                for r in spot(i)
+            ],
+            axis=0,
+        )
+        s = jnp.dot(keys, q_ref[h], preferred_element_type=F32) + bias[i]
+        scores[h % 4, i] = s
+        return jnp.maximum(top, jnp.max(s.reshape(-1, 8, wide), axis=0))
+
+    def weigh(h, i, top, total):
+        w = jnp.exp2((scores[h % 4, i] - top) * log2)
+        weights[h % 4, i] = w.astype(BF16)
+        return total + jnp.sum(w.reshape(-1, 8, wide), axis=0)
+
+    def mix(h, i):
+        cols = slice(h * VD, (h + 1) * VD)
+        values = jnp.concatenate([vt_ref[cols, pl.ds(r, BLK)] for r in spot(i)], axis=1)
+        acc[h % 2] += jnp.dot(values, weights[h % 4, i], preferred_element_type=F32)
+
+    low_top = jnp.full((8, wide), masked_value, F32)
+    zero = jnp.zeros((8, wide), F32)
+    tops, totals, sums = {}, {}, {}
+    for stage in range(0, heads + 4, 2):
+        scored = [h for h in (stage, stage + 1) if h < heads]
+        weighed = [h for h in (stage - 2, stage - 1) if 0 <= h < heads]
+        mixed = [h for h in (stage - 4, stage - 3) if 0 <= h < heads]
+        for h in weighed:
+            tops[h] = jnp.max(tops[h], axis=0, keepdims=True)
+            max_ref[h : h + 1, :] = jnp.maximum(tops[h][:, :BLK], tops[h][:, BLK:]) * scale
+        if mixed:
+            acc[...] = jnp.zeros_like(acc)
+
+        def body(i, carry):
+            found, added = carry
+            for h in mixed:
+                mix(h, i)
+            added = [weigh(h, i, tops[h], t) for h, t in zip(weighed, added)]
+            found = [score(h, i, t) for h, t in zip(scored, found)]
+            return found, added
+
+        found, added = lax.fori_loop(
+            0, count, body, ([low_top for h in scored], [zero for h in weighed])
+        )
+        tops.update(zip(scored, found))
+        totals.update(zip(weighed, added))
+        for h in mixed:
+            total = jnp.sum(totals[h], axis=0, keepdims=True)
+            out_ref[0, :, h * VD : (h + 1) * VD] = (acc[h % 2] / total).T.astype(BF16)
+
+
+def attend(block_order, segment_ids, q_all, k_all, vt_all, kr_all):
+    heads, _, tokens = q_all.shape
+    vmem, smem = pl.BlockSpec(memory_space=pltpu.VMEM), pl.BlockSpec(memory_space=pltpu.SMEM)
+    return pl.pallas_call(
+        attention_kernel,
+        out_shape=(
+            jax.ShapeDtypeStruct((1, tokens, heads * VD), BF16),
+            jax.ShapeDtypeStruct((heads, BLK), F32),
+        ),
+        in_specs=[smem, smem, vmem, vmem, vmem, vmem, vmem],
+        out_specs=(vmem, vmem),
+        scratch_shapes=[
+            pltpu.SMEM((block_order.shape[1],), jnp.int32),
+            pltpu.SMEM((block_order.shape[1] + 8,), jnp.int32),
+            pltpu.SMEM((block_order.shape[1] + 8,), jnp.int32),
+            pltpu.VMEM((block_order.shape[1] // RUN, RUN * BLK, tokens), F32),
+            pltpu.VMEM((4, block_order.shape[1] // RUN, RUN * BLK, tokens), F32),
+            pltpu.VMEM((4, block_order.shape[1] // RUN, RUN * BLK, tokens), BF16),
+            pltpu.VMEM((2, VD, tokens), F32),
+        ],
+        compiler_params=pltpu.CompilerParams(vmem_limit_bytes=40 * MIB),
+        name="attend",
+    )(
+        block_order, segment_ids, segment_ids.reshape(-1, BLK),
+        *(pltpu.with_memory_space_constraint(v, pltpu.VMEM) for v in (q_all, k_all, vt_all, kr_all)),
+    )
 
 
 def exchange_kernel(nseq, ndp, max_ref, out_ref, mine, got, ssem, rsem, lsem):
@@ -475,48 +508,32 @@
             pltpu.VMEM((total, heads * NOPE), BF16),
             pltpu.VMEM((heads * VD, total), BF16),
             pltpu.VMEM((total, 2 * ROPE), BF16),
-            pltpu.VMEM((heads, tokens, 256), BF16),
+            pltpu.VMEM((heads, 256, tokens), BF16),
         ),
-        in_specs=[smem, vmem, vmem, anyw, anyw, anyw, anyw],
+        in_specs=[smem, vmem, anyw, anyw, anyw, anyw, anyw],
         out_specs=(vmem, vmem, vmem, vmem),
         scratch_shapes=[
             pltpu.VMEM((nseq, *w_uq.shape), BF16),
             pltpu.VMEM((nseq, *w_uk.shape), BF16),
             pltpu.VMEM((nseq, *w_uv.shape), BF16),
-            pltpu.VMEM((NTP, 2, NZ, BLK, 2 * key_latent.shape[2]), BF16),
-            pltpu.VMEM((2, NZ, BLK, 2 * ROPE), BF16),
-            pltpu.VMEM((NTP, tokens, query_latent.shape[2]), BF16),
+            pltpu.VMEM((NTP, 2, NZ, key_latent.shape[2], tokens), BF16),
+            pltpu.VMEM((2, NZ, ROPE, tokens), BF16),
+            pltpu.VMEM((NTP, query_latent.shape[2], tokens), BF16),
             pltpu.VMEM((w_uv.shape[1], nseq * w_uv.shape[0]), BF16),
-            pltpu.VMEM((2, tokens, 2 * ROPE), F32),
+            pltpu.VMEM((2, ROPE // 2, tokens), F32),
             pltpu.SemaphoreType.DMA((160,)),
             pltpu.SemaphoreType.DMA((160,)),
-            pltpu.SemaphoreType.DMA((4,)),
+            pltpu.SemaphoreType.DMA((5,)),
         ],
         compiler_params=pltpu.CompilerParams(
             collective_id=0, has_side_effects=True, vmem_limit_bytes=40 * MIB
         ),
         name="gather",
-    )(block_order, rope_key, key_latent, query_latent, w_uq, w_uk, w_uv)
-    context, row_max = pl.pallas_call(
-        attention_kernel,
-        out_shape=(
-            jax.ShapeDtypeStruct((1, tokens, heads * VD), BF16),
-            jax.ShapeDtypeStruct((heads, BLK), F32),
-        ),
-        in_specs=[smem, smem, vmem, vmem, vmem, vmem, vmem],
-        out_specs=(vmem, vmem),
-        scratch_shapes=[
-            pltpu.SMEM((block_order.shape[1],), jnp.int32),
-            pltpu.VMEM((heads, VD, BLK), F32),
-            pltpu.VMEM((heads, BLK), F32),
-            pltpu.VMEM((heads, BLK), F32),
-        ],
-        compiler_params=pltpu.CompilerParams(vmem_limit_bytes=32 * MIB),
-        name="attend",
     )(
-        block_order, segment_ids, segment_ids.reshape(-1, BLK),
-        q_all, k_all, vt_all, kr_all,
+        block_order, jnp.swapaxes(rope_key, 1, 2), jnp.swapaxes(key_latent, 1, 2),
+        jnp.swapaxes(query_latent, 1, 2), w_uq, w_uk, w_uv,
     )
+    context, row_max = attend(block_order, segment_ids, q_all, k_all, vt_all, kr_all)
     n = nseq * ndp - 1
     best = pl.pallas_call(
         functools.partial(exchange_kernel, nseq, ndp),

time: 130 us -> 93.7 us (0.72); the launches traced: 132 us -> 93.2 us
  local copies, waits for them, and re-layouts: 20.1 us -> 0.3 us
  Pallas kernels: 109 us -> 90 us
    unnamed x21 -> x4, local copies, waits for them, and re-layouts: 19.8 us -> 0.01 us
    pallas_call x1, Pallas kernels: 25.4 us -> 15.2 us  [attend(): pl.pallas_call(attention_kernel, out_shape=(jax.ShapeDtypeStruct((1, toke...]
    pallas_call x1, Pallas kernels: 22.2 us -> 14.9 us  [on_device(): pl.pallas_call(functools.partial(exchange_kernel, nseq, ndp), out_shape=j...]
where the time goes in v2:
time: 93.7 us; the launch traced here: 93.2 us
  Pallas kernels  90 us (96%)
  other arithmetic  2.23 us (2%)
    pallas_call x1, Pallas kernels, on_device(): pl.pallas_call(gather_kernel, out_shape=(pltpu.VMEM((total, heads * NOPE)...  60 us
    pallas_call x1, Pallas kernels, attend(): pl.pallas_call(attention_kernel, out_shape=(jax.ShapeDtypeStruct((1, toke...  15.2 us
    pallas_call x1, Pallas kernels, on_device(): pl.pallas_call(functools.partial(exchange_kernel, nseq, ndp), out_shape=j...  14.9 us

profile of v2, /device:TPU:1, one launch (start us, length us, event | category | flops | bytes accessed | tf_op | source)
XLA Modules:
  0.0 93.2 jit_solution(16773705629480219631)
XLA Ops:
  0.6 60.0 %gather.1 = (bf16[4096,1024]{1,0:T(8,128)(2,1)S(1)}, bf16[1024,4096]{1,0:T(8,128)(2,1)S(1)}, bf16[4096,128]{1,0:T(8,128)(2,1)S(1)}, bf16[8,256,256]{2,1,0:T(8,128)(2,1)S(1)}) custom-call(s32[1,32]{1,0:T(1,128)} %order.3, bf16[1,64,256]{2,1,0:T(8,128)(2,1)} %bitcast.8, bf16[1,64,256]{2,1,0:T(8,128)(2,1)} %bitcast.9, bf16[1,192,256]{2,1,0:T(8,128)(2,1)} %bitcast.6, ...), custom_call_target="tpu_custom_call" | custom-call | tf_op jit(solution)/shard_map/gather/pallas_call | solution.py:505
  60.6 0.0 copy-start.1
  60.6 0.0 copy-start
  60.6 15.2 %attend.1 = (bf16[1,256,1024]{2,1,0:T(8,128)(2,1)}, f32[8,128]{1,0:T(8,128)}) custom-call(s32[1,32]{1,0:T(1,128)} %order.3, s32[1,4096]{1,0:T(1,128)} %segs.1, s32[32,128]{1,0:T(8,128)} %bitcast.7, bf16[8,256,256]{2,1,0:T(8,128)(2,1)S(1)} %get-tuple-element.9.q_ref, bf16[4096,1024]{1,0:T(8,128)(2,1)S(1)} %get-tuple-element.10.k_ref, ...), custom_call_target="tpu_custom_call" | custom-call | tf_op jit(solution)/shard_map/attend/pallas_call | solution.py:441
  75.8 14.9 %exchange.1 = f32[8,128]{1,0:T(8,128)} custom-call(f32[8,128]{1,0:T(8,128)} %get-tuple-element.14.max_ref), custom_call_target="tpu_custom_call" | custom-call | tf_op jit(solution)/shard_map/exchange/pallas_call | solution.py:538
  90.7 0.8 reduce_max.9
  91.5 0.1 broadcast_in_dim.5
  91.6 0.1 broadcast_bitcast_fusion
  91.7 0.1 broadcast_in_dim.4
  91.7 0.1 mul.20
  91.8 0.0 copy-done.1
  91.8 0.7 multiply_convert_fusion.1
  92.5 0.0 copy-done
  92.5 0.8 multiply_convert_fusion
  (2 shorter events, 0.0 us)
Async XLA Ops:
  60.6 31.2 %copy-start.1 = (bf16[32,1024]{1,0:T(8,128)(2,1)S(1)}, bf16[32,1024]{1,0:T(8,128)(2,1)}, u32[]{:S(2)}) copy-start(bf16[32,1024]{1,0:T(8,128)(2,1)} %uk_hbm.1) | copy-start | bytes 196612
  60.6 31.9 %copy-start = (bf16[96,1536]{1,0:T(8,128)(2,1)S(1)}, bf16[96,1536]{1,0:T(8,128)(2,1)}, u32[]{:S(2)}) copy-start(bf16[96,1536]{1,0:T(8,128)(2,1)} %uq_hbm.1) | copy-start | bytes 884740
